TPU v7x, 32 devices: a whole 2x2x4 slice. The times are simulated.
32 devices in a mesh: pq: 2 (over x), rs: 16 (over z, y, core).
Axes of the slice: x: 2, y: 2, z: 4, core: 2. Of those that a mesh axis runs over, the one named last changes fastest.
Arguments:
- integrals: bfloat16 [128, 1152, 1152], P('pq', 'rs'), may hold values from -6 to 6
- coeff: bfloat16 [1152, 896], P('rs', 'pq'), may hold values from -0.1875 to 0.1875
Outputs:
- half_mo: bfloat16 [128, 896, 896], P('pq', 'rs')
All inputs are finite; a program needn't handle non-finite values.
Results may differ from a plain program's by a relative error of at most 0.0049.
Values may be sent and summed in bfloat16 or wider, within the bound.
A program may use at most 128 MiB of HBM per device.

v0:
```python
import jax
import jax.numpy as jnp
from jax import lax
from jax.sharding import PartitionSpec as P

NBASIS = 1152
NORB = 896


def second_half(received, panel):
    return jnp.einsum("prl,rk->plk", received, panel, preferred_element_type=jnp.float32).astype(
        jnp.bfloat16
    )


def on_device(integrals, coeff):
    pair_rows = integrals.shape[0]
    block_rows = integrals.shape[1]
    flat = integrals.reshape(pair_rows * block_rows, NBASIS)
    strip = lax.all_gather(coeff, "pq", axis=1, tiled=True)
    panel = lax.all_gather(strip, "rs", axis=0, tiled=True)
    first = jnp.dot(flat, panel, preferred_element_type=jnp.float32).astype(jnp.bfloat16)
    first = first.reshape(pair_rows, block_rows, NORB)
    return second_half(lax.all_to_all(first, "rs", split_axis=2, concat_axis=1, tiled=True), panel)


def solution(mesh):
    placed = (P("pq", "rs", None), P("rs", "pq"))
    return jax.shard_map(
        on_device, mesh=mesh, in_specs=placed, out_specs=P("pq", "rs", None), check_vma=False
    )
```

profile of v0, /device:TPU:1, one launch (start us, length us, event | category | flops | bytes accessed | tf_op | source)
XLA Modules:
  0.0 468.6 jit_solution(1243256376461925950)
XLA Ops:
  6.5 0.0 all-gather.3.cloned.1.call-start
  6.5 4.7 %all-gather = bf16[2,448,72]{1,2,0:T(8,128)(2,1)S(1)} all-gather(bf16[1,448,72]{1,2,0:T(8,128)(2,1)} %bitcast.25), channel_id=1, replica_groups=mesh['pq'=2,'rs'=16] {'pq'}, dimensions={0}, use_global_device_ids=true | all-gather | bytes 193536 | tf_op jit(solution)/shard_map/all_gather | solution.py:20
  11.2 0.1 copy.7
  11.3 0.8 reshape.9
  12.1 0.0 all-gather.3.cloned.1.call-update
  12.2 44.5 %all-gather.3.cloned.1.call-done = bf16[1152,896]{1,0:T(8,128)(2,1)} async-done(((bf16[72,896]{1,0:T(8,128)(2,1)}), bf16[1152,896]{1,0:T(8,128)(2,1)}) %all-gather.3.cloned.1.call-update) | async-done | bytes 2064400 | tf_op jit(solution)/shard_map/all_gather | solution.py:21
  56.7 17.5 %convolution_convert_fusion = bf16[4608,896]{1,0:T(8,128)(2,1)} fusion(bf16[4608,1152]{1,0:T(8,128)(2,1)} %bitcast.26, bf16[1152,896]{1,0:T(8,128)(2,1)} %all-gather.3.cloned.1.call-done), kind=kOutput, calls=%fused_computation | convolution fusion | flops 9516810240 | bytes 20938752 | tf_op jit(solution)/shard_map/dot_general | solution.py:22
  74.2 18.5 %copy.8 = bf16[64,72,896]{1,0,2:T(8,128)(2,1)} copy(bf16[64,72,896]{2,1,0:T(8,128)(2,1)} %bitcast.23) | data formatting | bytes 16515072 | tf_op jit(solution)/shard_map/reshape | solution.py:23
  92.7 321.5 %all_to_all.18 = bf16[64,72,896]{1,0,2:T(8,128)(2,1)S(1)} all-to-all(bf16[64,72,896]{1,0,2:T(8,128)(2,1)} %copy.8), channel_id=1, replica_groups=mesh['pq'=2,'rs'=16] {'rs'}, dimensions={2} | all-to-all | bytes 16515072 | tf_op jit(solution)/shard_map/all_to_all | solution.py:24
  414.1 10.6 %copy.10 = bf16[64,16,72,56]{2,1,3,0:T(8,128)(2,1)} copy(bf16[64,16,72,56]{2,0,3,1:T(8,128)(2,1)S(1)} %bitcast.22) | data formatting | bytes 16515072 | tf_op jit(solution)/shard_map/all_to_all | solution.py:24
  424.7 0.0 copy-start
  424.7 23.2 %all_to_all.16 = bf16[64,1152,56]{1,2,0:T(8,128)(2,1)} reshape(bf16[64,16,72,56]{2,1,3,0:T(8,128)(2,1)} %copy.10) | data formatting | bytes 16515072 | tf_op jit(solution)/shard_map/all_to_all | solution.py:24
  447.9 0.0 copy-done
  447.9 13.8 %convolution_convert_fusion.1 = bf16[64,56,896]{2,1,0:T(8,128)(2,1)} fusion(bf16[64,1152,56]{1,2,0:T(8,128)(2,1)} %all_to_all.16, bf16[1152,896]{1,0:T(8,128)(2,1)S(1)} %copy-done), kind=kOutput, calls=%fused_computation.1 | convolution fusion | flops 7401963520 | bytes 16744448 | tf_op jit(solution)/shard_map/prl,rk->plk/dot_general | solution.py:11
Async XLA Ops:
  6.5 50.2 %all-gather.3.cloned.1.call-start = ((), (), s32[]{:S(2)}) async-start(), calls=%async_computation.1 | async-start | bytes 2193408 | tf_op jit(solution)/shard_map/all_gather | solution.py:21
  424.7 23.2 %copy-start = (bf16[1152,896]{1,0:T(8,128)(2,1)S(1)}, bf16[1152,896]{1,0:T(8,128)(2,1)}, u32[]{:S(2)}) copy-start(bf16[1152,896]{1,0:T(8,128)(2,1)} %all-gather.3.cloned.1.call-done) | copy-start | bytes 6193156
Sparse Core Ops, SparseCore 0:
  12.3 44.3 all-gather.2
where the time goes:
time: 470 us; the launch traced here: 469 us
  blocking collectives  326 us (69%)
  local copies, waits for them, and re-layouts  53.2 us (11%)
  waiting for transfers between devices  44.6 us (9%)
  matrix products  31.3 us (7%)
  between operations  13.4 us (3%)
    all_to_all x1, blocking collectives, on_device(): lax.all_to_all(first, 'rs', split_axis=2, concat_axis=1, tiled=True)  321 us
    all_gather x1, waiting for transfers between devices, on_device(): panel = lax.all_gather(strip, 'rs', axis=0, tiled=True)  44.5 us
    all_to_all x2, local copies, waits for them, and re-layouts, on_device(): lax.all_to_all(first, 'rs', split_axis=2, concat_axis=1, tiled=True)  33.8 us
    reshape x1, local copies, waits for them, and re-layouts, on_device(): first = first.reshape(pair_rows, block_rows, NORB)  18.5 us
    dot_general x1, matrix products, on_device(): jnp.dot(flat, panel, preferred_element_type=jnp.float32)  17.5 us
    dot_general x1, matrix products, second_half(): jnp.einsum('prl,rk->plk', received, panel, preferred_element_type=jnp.flo...  13.8 us
  transfers between devices with their start and end apart: 1, of which 1 were waited for; matrix products, arithmetic and copies ran while one was open for 0% of the time, Pallas kernels for 0%

commit v1 on v0

--- a/solution.py
+++ b/solution.py
@@ -21,7 +21,18 @@
     panel = lax.all_gather(strip, "rs", axis=0, tiled=True)
     first = jnp.dot(flat, panel, preferred_element_type=jnp.float32).astype(jnp.bfloat16)
     first = first.reshape(pair_rows, block_rows, NORB)
-    return second_half(lax.all_to_all(first, "rs", split_axis=2, concat_axis=1, tiled=True), panel)
+    return second_half(
+        jnp.concatenate(
+            lax.all_to_all(
+                jnp.stack(jnp.split(first, lax.axis_size("rs"), 2), 0),
+                axis_name="rs",
+                split_axis=0,
+                concat_axis=0,
+            ),
+            1,
+        ),
+        panel,
+    )
 
 
 def solution(mesh):

time: 470 us -> 511 us (1.087)
  local copies, waits for them, and re-layouts: 53.2 us -> 97.4 us
    unnamed x3 -> x52, local copies, waits for them, and re-layouts: 0.8 us -> 46.2 us
    all_to_all x2 -> x0, local copies, waits for them, and re-layouts: 33.8 us -> none  [on_device(): lax.all_to_all(first, 'rs', split_axis=2, concat_axis=1, tiled=True)]
    reshape x1 -> x2, local copies, waits for them, and re-layouts: 18.5 us -> 42.7 us  [on_device(): jnp.concatenate(lax.all_to_all(jnp.stack(jnp.split(first, lax.axis_size('...]
    split x0 -> x1, local copies, waits for them, and re-layouts: none -> 8.3 us  [on_device(): jnp.split(first, lax.axis_size('rs'), 2)]
where the time goes in v1:
time: 511 us; the launch traced here: 510 us
  blocking collectives  325 us (64%)
  local copies, waits for them, and re-layouts  97.4 us (19%)
  waiting for transfers between devices  44.6 us (9%)
  matrix products  28.9 us (6%)
  between operations  13.6 us (3%)
    all_to_all x1, blocking collectives, on_device(): lax.all_to_all(jnp.stack(jnp.split(first, lax.axis_size('rs'), 2), 0), ax...  321 us
    unnamed x52, local copies, waits for them, and re-layouts  46.2 us
    all_gather x1, waiting for transfers between devices, on_device(): panel = lax.all_gather(strip, 'rs', axis=0, tiled=True)  44.5 us
    reshape x2, local copies, waits for them, and re-layouts, on_device(): jnp.concatenate(lax.all_to_all(jnp.stack(jnp.split(first, lax.axis_size('...  42.7 us
    dot_general x1, matrix products, on_device(): jnp.dot(flat, panel, preferred_element_type=jnp.float32)  15.1 us
    dot_general x1, matrix products, second_half(): jnp.einsum('prl,rk->plk', received, panel, preferred_element_type=jnp.flo...  13.8 us
  transfers between devices with their start and end apart: 1, of which 1 were waited for; matrix products, arithmetic and copies ran while one was open for 0% of the time, Pallas kernels for 0%

profile of v1, /device:TPU:1, one launch (start us, length us, event | category | flops | bytes accessed | tf_op | source)
XLA Modules:
  0.0 510.0 jit_solution(11067591270855484033)
XLA Ops:
  6.5 4.7 all-gather
  11.3 0.8 reshape.17
  12.2 44.5 %all-gather.3.cloned.1.call-done = bf16[1152,896]{1,0:T(8,128)(2,1)} async-done(((bf16[72,896]{1,0:T(8,128)(2,1)}), bf16[1152,896]{1,0:T(8,128)(2,1)}) %all-gather.3.cloned.1.call-update) | async-done | bytes 2064400 | tf_op jit(solution)/shard_map/all_gather | solution.py:21
  56.7 15.1 %convolution_convert_fusion = bf16[4608,896]{1,0:T(8,128)(2,1)S(1)} fusion(bf16[4608,1152]{1,0:T(8,128)(2,1)} %bitcast.55, bf16[1152,896]{1,0:T(8,128)(2,1)} %all-gather.3.cloned.1.call-done), kind=kOutput, calls=%fused_computation | convolution fusion | flops 9516810240 | bytes 20938752 | tf_op jit(solution)/shard_map/dot_general | solution.py:22
  71.8 8.3 %fusion.1 = (bf16[64,72,56]{2,1,0:T(8,128)(2,1)}, bf16[64,72,56]{2,1,0:T(8,128)(2,1)}, bf16[64,72,56]{2,1,0:T(8,128)(2,1)}, bf16[64,72,56]{2,1,0:T(8,128)(2,1)},...) fusion(bf16[64,72,896]{2,1,0:T(8,128)(2,1)S(1)} %bitcast.52), kind=kLoop, calls=%fused_computation.19 | loop fusion | bytes 16515072 | tf_op jit(solution)/shard_map/split | solution.py:27
  80.1 2.3 copy.38
  82.5 2.3 copy.37
  84.8 2.3 copy.36
  87.0 2.3 copy.35
  89.3 2.3 copy.34
  91.6 2.3 copy.33
  93.9 2.3 copy.32
  96.2 2.3 copy.31
  98.5 2.3 copy.30
  100.8 2.3 copy.29
  103.1 2.3 copy.28
  105.4 2.3 copy.27
  107.7 2.3 copy.26
  110.0 2.3 copy.25
  112.2 1.3 copy.24
  113.6 1.3 copy.23
  114.9 1.4 bitcast_dynamic-update-slice_fusion.15
  116.3 1.6 bitcast_dynamic-update-slice_fusion.14
  117.9 1.3 bitcast_dynamic-update-slice_fusion.13
  119.2 1.3 bitcast_dynamic-update-slice_fusion.12
  120.6 1.3 bitcast_dynamic-update-slice_fusion.11
  121.9 1.3 bitcast_dynamic-update-slice_fusion.10
  123.2 1.3 bitcast_dynamic-update-slice_fusion.9
  125.9 320.8 %all_to_all.5 = bf16[16,64,72,56]{2,3,1,0:T(8,128)(2,1)S(1)} all-to-all(bf16[16,64,72,56]{2,3,1,0:T(8,128)(2,1)S(1)} %bitcast_dynamic-update-slice_fusion), channel_id=1, replica_groups=mesh['pq'=2,'rs'=16] {'rs'}, dimensions={0} | all-to-all | bytes 16515072 | tf_op jit(solution)/shard_map/all_to_all | solution.py:26
  446.7 19.5 %copy.22 = bf16[64,16,72,56]{2,1,3,0:T(8,128)(2,1)} copy(bf16[64,16,72,56]{2,3,0,1:T(8,128)(2,1)S(1)} %bitcast.51) | data formatting | bytes 16515072 | tf_op jit(solution)/shard_map/reshape | solution.py:25
  466.2 23.2 %reshape.15 = bf16[64,1152,56]{1,2,0:T(8,128)(2,1)} reshape(bf16[64,16,72,56]{2,1,3,0:T(8,128)(2,1)} %copy.22) | data formatting | bytes 16515072 | tf_op jit(solution)/shard_map/reshape | solution.py:25
  489.4 13.8 %convolution_convert_fusion.1 = bf16[64,56,896]{2,1,0:T(8,128)(2,1)} fusion(bf16[64,1152,56]{1,2,0:T(8,128)(2,1)} %reshape.15, bf16[1152,896]{1,0:T(8,128)(2,1)S(1)} %copy-done.9), kind=kOutput, calls=%fused_computation.1 | convolution fusion | flops 7401963520 | bytes 16744448 | tf_op jit(solution)/shard_map/prl,rk->plk/dot_general | solution.py:11
  (32 shorter events, 1.4 us)
Async XLA Ops:
  6.5 50.2 %all-gather.3.cloned.1.call-start = ((), (), s32[]{:S(2)}) async-start(), calls=%async_computation.1 | async-start | bytes 2193408 | tf_op jit(solution)/shard_map/all_gather | solution.py:21
  113.6 11.7 %copy-start.3 = (bf16[64,72,56]{1,2,0:T(8,128)(2,1)S(1)}, bf16[64,72,56]{1,2,0:T(8,128)(2,1)}, u32[]{:S(2)}) copy-start(bf16[64,72,56]{1,2,0:T(8,128)(2,1)} %copy.35) | copy-start | bytes 1548292
  113.6 11.9 %copy-start.2 = (bf16[64,72,56]{1,2,0:T(8,128)(2,1)S(1)}, bf16[64,72,56]{1,2,0:T(8,128)(2,1)}, u32[]{:S(2)}) copy-start(bf16[64,72,56]{1,2,0:T(8,128)(2,1)} %copy.36) | copy-start | bytes 1548292
  114.9 9.6 %copy-start.8 = (bf16[64,72,56]{1,2,0:T(8,128)(2,1)S(1)}, bf16[64,72,56]{1,2,0:T(8,128)(2,1)}, u32[]{:S(2)}) copy-start(bf16[64,72,56]{1,2,0:T(8,128)(2,1)} %copy.30) | copy-start | bytes 1548292
  114.9 9.8 %copy-start.7 = (bf16[64,72,56]{1,2,0:T(8,128)(2,1)S(1)}, bf16[64,72,56]{1,2,0:T(8,128)(2,1)}, u32[]{:S(2)}) copy-start(bf16[64,72,56]{1,2,0:T(8,128)(2,1)} %copy.31) | copy-start | bytes 1548292
  114.9 9.9 %copy-start.6 = (bf16[64,72,56]{1,2,0:T(8,128)(2,1)S(1)}, bf16[64,72,56]{1,2,0:T(8,128)(2,1)}, u32[]{:S(2)}) copy-start(bf16[64,72,56]{1,2,0:T(8,128)(2,1)} %copy.32) | copy-start | bytes 1548292
  114.9 10.1 %copy-start.5 = (bf16[64,72,56]{1,2,0:T(8,128)(2,1)S(1)}, bf16[64,72,56]{1,2,0:T(8,128)(2,1)}, u32[]{:S(2)}) copy-start(bf16[64,72,56]{1,2,0:T(8,128)(2,1)} %copy.33) | copy-start | bytes 1548292
  114.9 10.2 %copy-start.4 = (bf16[64,72,56]{1,2,0:T(8,128)(2,1)S(1)}, bf16[64,72,56]{1,2,0:T(8,128)(2,1)}, u32[]{:S(2)}) copy-start(bf16[64,72,56]{1,2,0:T(8,128)(2,1)} %copy.34) | copy-start | bytes 1548292
  114.9 10.7 %copy-start.1 = (bf16[64,72,56]{1,2,0:T(8,128)(2,1)S(1)}, bf16[64,72,56]{1,2,0:T(8,128)(2,1)}, u32[]{:S(2)}) copy-start(bf16[64,72,56]{1,2,0:T(8,128)(2,1)} %copy.37) | copy-start | bytes 1548292
  116.3 9.4 %copy-start = (bf16[64,72,56]{1,2,0:T(8,128)(2,1)S(1)}, bf16[64,72,56]{1,2,0:T(8,128)(2,1)}, u32[]{:S(2)}) copy-start(bf16[64,72,56]{1,2,0:T(8,128)(2,1)} %copy.38) | copy-start | bytes 1548292
  466.2 23.2 %copy-start.9 = (bf16[1152,896]{1,0:T(8,128)(2,1)S(1)}, bf16[1152,896]{1,0:T(8,128)(2,1)}, u32[]{:S(2)}) copy-start(bf16[1152,896]{1,0:T(8,128)(2,1)} %all-gather.3.cloned.1.call-done) | copy-start | bytes 6193156
Sparse Core Ops, SparseCore 0:
  12.3 44.3 all-gather.2
